TPU v7x, 32 devices: a whole 2x2x4 slice. The times are simulated.
32 devices in a mesh: dp: 8 (over z, y), tensor: 4 (over x, core).
Axes of the slice: x: 2, y: 2, z: 4, core: 2. Of those that a mesh axis runs over, the one named last changes fastest.
Arguments:
- tokens: bfloat16 [16384, 1536], P('dp', 'tensor'), may hold values from -6 to 6
- segments: int32 [16384], P('dp'), may hold values from 0 to 5, as said below
- prenorm: float32 [1536], replicated, may hold values from 0.5 to 1.5
- gating: bfloat16 [1536, 3072], P(None, 'tensor'), may hold values from -0.15625 to 0.15625
- signal: bfloat16 [1536, 3072], P(None, 'tensor'), may hold values from -0.15625 to 0.15625
- memory: bfloat16 [1536, 256], replicated, may hold values from -0.15625 to 0.15625
- timestep: bfloat16 [1536, 48], P(None, 'tensor'), may hold values from -0.15625 to 0.15625
- kernel: float32 [4, 3072], P(None, 'tensor'), may hold values from -3 to 3
- offsets: float32 [3072], P('tensor'), may hold values from -0.5 to 0.5
- window: float32 [4, 256], replicated, may hold values from -3 to 3
- shifts: float32 [256], replicated, may hold values from -0.5 to 0.5
- baseline: float32 [48], P('tensor'), may hold values from -6.9 to -2.3
- decays: float32 [48], P('tensor'), may hold values from 0 to 2.77
- shortcut: float32 [48], P('tensor'), may hold values from 0.5 to 1.5
- postnorm: float32 [3072], P('tensor'), may hold values from 0.5 to 1.5
- readout: bfloat16 [3072, 1536], P('tensor'), may hold values from -0.109375 to 0.109375
- cotangent: bfloat16 [16384, 1536], P('dp', 'tensor'), may hold values from -6 to 6
Outputs:
- result: bfloat16 [16384, 1536], P('dp', 'tensor')
- tokens_gradient: float32 [16384, 1536], P('dp', 'tensor')
- prenorm_gradient: float32 [1536], P('tensor')
- gating_gradient: float32 [1536, 3072], P(None, 'tensor')
- signal_gradient: float32 [1536, 3072], P(None, 'tensor')
- memory_gradient: float32 [1536, 256], P('tensor')
- timestep_gradient: float32 [1536, 48], P(None, 'tensor')
- kernel_gradient: float32 [4, 3072], P(None, 'tensor')
- offsets_gradient: float32 [3072], P('tensor')
- window_gradient: float32 [4, 256], replicated
- shifts_gradient: float32 [256], replicated
- baseline_gradient: float32 [48], P('tensor')
- decays_gradient: float32 [48], P('tensor')
- shortcut_gradient: float32 [48], P('tensor')
- postnorm_gradient: float32 [3072], P('tensor')
- readout_gradient: float32 [3072, 1536], P('tensor')
Inputs may be any that keep to these rules, and one draw needn't show every extreme that they name: `segments`: within each sequence of 1024 consecutive tokens the numbers start at 0 and rise by one where a new document starts; documents hold 200 to 1000 tokens, except that the last one of a sequence may be shorter.
All inputs are finite; a program needn't handle non-finite values.
Results may differ from a plain program's by a relative error of at most 0.0082.
Values may be sent and summed in bfloat16 or wider, within the bound.
A program may use at most 384 MiB of HBM per device.

v0:
```python
from functools import partial

import jax
import jax.numpy as jnp
from jax import lax
from jax.sharding import PartitionSpec as P

D = 1536
SPAN = 256
SEQLEN = 1024
INNER = 3072


epsilon = 1e-05
highest = lax.Precision.HIGHEST


def causal_filter(values, weight, offset, segment):
    length = values.shape[1]
    summed = offset + weight[0] * values
    for lag_steps in range(1, weight.shape[0]):
        shifted = jnp.pad(values, ((0, 0), (lag_steps, 0), (0, 0)))[:, :length]
        earlier = jnp.pad(segment, ((0, 0), (lag_steps, 0)), constant_values=-1)[:, :length]
        matched = (earlier == segment).astype(jnp.float32)[:, :, None]
        summed = summed + weight[lag_steps] * shifted * matched
    return summed


def span_scan(signal_heads, stepsize, logdecay, writes, reads, segment):
    batches = signal_heads.shape[0]
    length = signal_heads.shape[1]
    heads_here = signal_heads.shape[2]
    head_width = signal_heads.shape[3]
    state_width = writes.shape[-1]
    blocks = length // SPAN

    def into_blocks(member):
        return jnp.swapaxes(member.reshape((batches, blocks, SPAN) + member.shape[2:]), 0, 1)

    lower_part = jnp.tril(jnp.ones((SPAN, SPAN), dtype=bool))

    def advance(carried_in, block_data):
        memory_state, last_segment = carried_in
        piece_signal, piece_step, piece_decay, piece_write, piece_read, piece_segment = block_data
        running = jnp.cumsum(piece_decay, axis=1)
        inside = lower_part[None] & (piece_segment[:, :, None] == piece_segment[:, None, :])
        inside_heads = inside[:, :, :, None]
        spread = running[:, :, None, :] - running[:, None, :, :]
        falloff = jnp.where(inside_heads, jnp.exp(jnp.where(inside_heads, spread, 0.0)), 0.0)
        scores = jnp.einsum("btn,bsn->bts", piece_read, piece_write, precision=highest)
        mixing = falloff * scores[:, :, :, None] * piece_step[:, None, :, :]
        output = jnp.einsum("btsh,bshp->bthp", mixing, piece_signal, precision=highest)
        carried = (piece_segment == last_segment[:, None]).astype(jnp.float32)
        entering = jnp.exp(running) * carried[:, :, None]
        output = (
            output
            + jnp.einsum("btn,bhpn->bthp", piece_read, memory_state, precision=highest)
            * entering[:, :, :, None]
        )
        tail_segment = piece_segment[:, -1]
        keeping = (piece_segment == tail_segment[:, None]).astype(jnp.float32)
        toward = jnp.exp(running[:, -1:, :] - running) * keeping[:, :, None] * piece_step
        persist = (
            jnp.exp(running[:, -1, :]) * (tail_segment == last_segment).astype(jnp.float32)[:, None]
        )
        memory_state = memory_state * persist[:, :, None, None] + jnp.einsum(
            "bsh,bshp,bsn->bhpn", toward, piece_signal, piece_write, precision=highest
        )
        return ((memory_state, tail_segment), output)

    starting = (
        jnp.zeros((batches, heads_here, head_width, state_width), jnp.float32),
        jnp.full((batches,), -1, jnp.int32),
    )
    block_inputs = (
        into_blocks(signal_heads),
        into_blocks(stepsize),
        into_blocks(logdecay),
        into_blocks(writes),
        into_blocks(reads),
        into_blocks(segment),
    )
    finished, outputs = lax.scan(advance, starting, block_inputs)
    return jnp.swapaxes(outputs, 0, 1).reshape(batches, length, heads_here, head_width)


def mixer(
    segment,
    gate_in,
    signal_in,
    memory_in,
    step_in,
    kernel,
    offsets,
    window,
    shifts,
    baseline,
    decays,
    shortcut,
):
    batches = segment.shape[0]
    length = segment.shape[1]
    signal_seq = jax.nn.silu(
        causal_filter(signal_in.reshape(batches, length, -1), kernel, offsets, segment)
    )
    memory_seq = jax.nn.silu(
        causal_filter(memory_in.reshape(batches, length, -1), window, shifts, segment)
    )
    state_width = memory_seq.shape[-1] // 2
    writes = memory_seq[..., :state_width]
    reads = memory_seq[..., state_width:]
    stepsize = jax.nn.softplus(step_in.reshape(batches, length, -1) + baseline)
    logdecay = -jnp.exp(decays) * stepsize
    heads_here = stepsize.shape[-1]
    signal_heads = signal_seq.reshape(batches, length, heads_here, -1)
    scanned = (
        span_scan(signal_heads, stepsize, logdecay, writes, reads, segment)
        + shortcut[:, None] * signal_heads
    )
    return scanned.reshape(batches * length, -1) * jax.nn.silu(gate_in)


def contract_rows(left_side, right_side):
    return lax.dot_general(
        left_side, right_side, (((0,), (0,)), ((), ())), preferred_element_type=jnp.float32
    )


def contract_cols(left_side, right_side):
    return lax.dot_general(
        left_side, right_side, (((1,), (1,)), ((), ())), preferred_element_type=jnp.float32
    )


def local(
    tokens,
    segments,
    prenorm,
    gating,
    signal,
    memory,
    timestep,
    kernel,
    offsets,
    window,
    shifts,
    baseline,
    decays,
    shortcut,
    postnorm,
    readout,
    cotangent,
):
    width_here = tokens.shape[1]
    position = lax.axis_index("tensor") * width_here
    gain_here = lax.dynamic_slice_in_dim(prenorm, position, width_here)
    tokens_wide = tokens.astype(jnp.float32)
    gathered = lax.all_gather(tokens, "tensor", axis=1, tiled=True)
    gathered_wide = gathered.astype(jnp.float32)
    inverse = lax.rsqrt(jnp.mean(gathered_wide * gathered_wide, axis=-1, keepdims=True) + epsilon)
    normed = (gathered_wide * inverse * prenorm).astype(jnp.bfloat16)
    scaled_rows = tokens_wide * inverse
    gate_in = jnp.dot(normed, gating, preferred_element_type=jnp.float32)
    signal_in = jnp.dot(normed, signal, preferred_element_type=jnp.float32)
    memory_in = jnp.dot(normed, memory, preferred_element_type=jnp.float32)
    step_in = jnp.dot(normed, timestep, preferred_element_type=jnp.float32)
    segment_rows = segments.reshape(-1, SEQLEN)
    mixed, mixer_pull = jax.vjp(
        partial(mixer, segment_rows),
        gate_in,
        signal_in,
        memory_in,
        step_in,
        kernel,
        offsets,
        window,
        shifts,
        baseline,
        decays,
        shortcut,
    )
    gate_squares = lax.psum(jnp.sum(mixed * mixed, axis=-1), "tensor")
    factor = lax.rsqrt(gate_squares[:, None] / INNER + epsilon)
    balanced = mixed * factor
    outnormed = (balanced * postnorm).astype(jnp.bfloat16)
    partial_out = jnp.dot(outnormed, readout, preferred_element_type=jnp.float32)
    summed_out = lax.psum_scatter(partial_out, "tensor", scatter_dimension=1, tiled=True)
    outcome = (tokens_wide + summed_out).astype(jnp.bfloat16)
    piece = lax.all_gather(cotangent, "tensor", axis=1, tiled=True)
    back_rows = contract_cols(piece, readout)
    update = contract_rows(outnormed, piece)
    readout_grad = update
    postnorm_grad = jnp.sum(back_rows * balanced, axis=0)
    balanced_back = back_rows * postnorm
    gate_dots = lax.psum(jnp.sum(balanced_back * balanced, axis=-1), "tensor")
    mixed_back = factor * (balanced_back - balanced * gate_dots[:, None] / INNER)
    (
        gate_back,
        signal_back,
        memory_back,
        step_back,
        kernel_grad,
        offsets_grad,
        window_grad,
        shifts_grad,
        baseline_grad,
        decays_grad,
        shortcut_grad,
    ) = mixer_pull(mixed_back)
    memory_back, window_grad, shifts_grad = lax.psum(
        (memory_back, window_grad, shifts_grad), "tensor"
    )
    gate_low = gate_back.astype(jnp.bfloat16)
    signal_low = signal_back.astype(jnp.bfloat16)
    memory_low = memory_back.astype(jnp.bfloat16)
    step_low = step_back.astype(jnp.bfloat16)
    gating_grad = contract_rows(normed, gate_low)
    signal_grad = contract_rows(normed, signal_low)
    timestep_grad = contract_rows(normed, step_low)
    normed_cols = lax.dynamic_slice_in_dim(normed, position, width_here, 1)
    memory_grad = contract_rows(normed_cols, memory_low)
    normed_part = (
        contract_cols(gate_low, gating)
        + contract_cols(signal_low, signal)
        + contract_cols(step_low, timestep)
    )
    normed_back = lax.psum_scatter(normed_part, "tensor", scatter_dimension=1, tiled=True)
    memory_rows = lax.dynamic_slice_in_dim(memory, position, width_here, 0)
    normed_back = normed_back + contract_cols(memory_low, memory_rows)
    scaled_back = normed_back * gain_here
    prenorm_grad = jnp.sum(normed_back * scaled_rows, axis=0)
    norm_dots = lax.psum(jnp.sum(scaled_back * scaled_rows, axis=-1), "tensor")
    tokens_grad = inverse * (scaled_back - scaled_rows * norm_dots[:, None] / D) + cotangent.astype(
        jnp.float32
    )
    (
        prenorm_grad,
        gating_grad,
        signal_grad,
        memory_grad,
        timestep_grad,
        kernel_grad,
        offsets_grad,
        window_grad,
        shifts_grad,
        baseline_grad,
        decays_grad,
        shortcut_grad,
        postnorm_grad,
        readout_grad,
    ) = lax.psum(
        (
            prenorm_grad,
            gating_grad,
            signal_grad,
            memory_grad,
            timestep_grad,
            kernel_grad,
            offsets_grad,
            window_grad,
            shifts_grad,
            baseline_grad,
            decays_grad,
            shortcut_grad,
            postnorm_grad,
            readout_grad,
        ),
        "dp",
    )
    return (
        outcome,
        tokens_grad,
        prenorm_grad,
        gating_grad,
        signal_grad,
        memory_grad,
        timestep_grad,
        kernel_grad,
        offsets_grad,
        window_grad,
        shifts_grad,
        baseline_grad,
        decays_grad,
        shortcut_grad,
        postnorm_grad,
        readout_grad,
    )


def solution(mesh):
    placed = (
        P("dp", "tensor"),
        P("dp"),
        P(),
        P(None, "tensor"),
        P(None, "tensor"),
        P(),
        P(None, "tensor"),
        P(None, "tensor"),
        P("tensor"),
        P(),
        P(),
        P("tensor"),
        P("tensor"),
        P("tensor"),
        P("tensor"),
        P("tensor", None),
        P("dp", "tensor"),
    )
    return jax.shard_map(
        local,
        mesh=mesh,
        in_specs=placed,
        out_specs=(
            P("dp", "tensor"),
            P("dp", "tensor"),
            P("tensor"),
            P(None, "tensor"),
            P(None, "tensor"),
            P("tensor", None),
            P(None, "tensor"),
            P(None, "tensor"),
            P("tensor"),
            P(),
            P(),
            P("tensor"),
            P("tensor"),
            P("tensor"),
            P("tensor"),
            P("tensor", None),
        ),
        check_vma=False,
    )
```

profile of v0, /device:TPU:0, one launch (start us, length us, event | category | flops | bytes accessed | tf_op | source)
XLA Modules:
  0.0 1599.4 jit_solution(2744719677325578071)
XLA Ops:
  14.9 43.8 %all-gather.3.cloned.1.call-done = bf16[2048,1536]{1,0:T(8,128)(2,1)} async-done(((bf16[2048,384]{1,0:T(8,128)(2,1)}), bf16[2048,1536]{1,0:T(8,128)(2,1)}) %all-gather.3.cloned.1.call-update) | async-done | bytes 6291472 | tf_op jit(solution)/shard_map/all_gather | solution.py:158
  85.6 16.3 %fusion.140 = (f32[2,1024,768]{1,2,0:T(8,128)}, f32[2,1024,768]{1,2,0:T(8,128)}) fusion(f32[2,1024]{1,0:T(2,128)S(1)} %get-tuple-element.2063, f32[2,1024,768]{1,2,0:T(8,128)} %copy.449, f32[768]{0:T(1024)S(1)} %get-tuple-element.1869, f32[2,1024]{1,0:T(2,128)S(1)} %get-tuple-element.2062, f32[768]{0:T(1024)S(1)} %get-tuple-element.1870, ...), kind=kLoop, calls=%fused_computation.229 | loop fusion | flops 23592960 | bytes 18914304 | tf_op jit(solution)/shard_map/jvp(jit(silu))/mul | solution.py:103
  137.6 249.4 %while.85 = (s32[]{:T(128)}, f32[2,12,64,128]{3,2,1,0:T(8,128)S(1)}, s32[2]{0:T(128)S(1)}, f32[4,2,256,12,64]{2,4,3,1,0:T(8,128)}, pred[4,2,256,256,12]{3,2,4,1,...) while((s32[]{:T(128)}, ...), condition=%wide.region_4.5_spmd.clone, body=%wide.region_1.4_spmd.clone.sunk | while | flops 2636685312 | bytes 51448588 | solution.py:83
  150.8 10.3 multiply_dynamic-update-slice_fusion.2
  166.4 9.8 bitcast_dynamic-update-slice_fusion.22
  213.2 10.2 multiply_dynamic-update-slice_fusion.2
  228.6 9.8 bitcast_dynamic-update-slice_fusion.22
  275.5 10.2 multiply_dynamic-update-slice_fusion.2
  290.9 9.9 bitcast_dynamic-update-slice_fusion.22
  337.8 10.1 multiply_dynamic-update-slice_fusion.2
  353.2 9.8 bitcast_dynamic-update-slice_fusion.22
  394.0 9.4 copy.458
  418.2 15.6 multiply_reduce_fusion.6
  440.0 11.6 multiply_reduce_fusion
  457.4 16.5 %fusion.138 = (f32[768]{0:T(1024)}, f32[2048,768]{1,0:T(8,128)}, bf16[2048,768]{1,0:T(8,128)(2,1)}) fusion(f32[2,1024,768]{2,1,0:T(8,128)} %copy.459, f32[2048,768]{1,0:T(8,128)} %get-tuple-element.2068, f32[2048]{0:T(1024)S(1)} %psum.141, f32[2048,768]{1,0:T(8,128)} %get-tuple-element.2023, f32[2048,768]{1,0:T(8,128)} %get-tuple-element.2069, ...), kind=kLoop, calls=%fused_computation.216 | loop fusion | flops 36175104 | bytes 40920064 | tf_op jit(solution)/shard_map/transpose(jvp())/reduce_sum | solution.py:118
  496.3 298.9 %while.86 = (s32[]{:T(128)}, f32[2,12,64,128]{3,2,1,0:T(8,128)S(1)}, f32[4,2,256,12,64]{2,4,3,1,0:T(8,128)}, f32[4,2,256,12]{3,1,2,0:T(2,128)}, f32[4,2,256,12]{...) while((s32[]{:T(128)}, ...), condition=%wide.region_20.21_spmd.clone, body=%wide.region_10.20_spmd.clone.sunk | while | flops 5257359360 | bytes 81208632 | solution.py:83
  503.2 14.1 fusion.266
  577.7 14.1 fusion.266
  652.3 14.1 fusion.266
  726.9 14.1 fusion.266
  767.2 8.8 bitcast_dynamic-update-slice_fusion.26
  797.7 10.4 copy.474
  823.1 17.2 %multiply_reduce_fusion.4 = (f32[768]{0:T(1024)S(1)}, f32[768]{0:T(1024)S(1)}, f32[768]{0:T(1024)S(1)}, f32[768]{0:T(1024)S(1)}, f32[768]{0:T(1024)S(1)}, /*index=5*/f32[2,1024,768]{1,2,0:T(8,128)S(1)}) fusion(f32[2,1024,768]{1,2,0:T(8,128)} %copy.449, f32[2,1024]{1,0:T(2,128)S(1)} %copy-done.27, f32[2,1024]{1,0:T(2,128)S(1)} %copy-done.25, ...), kind=kLoop, calls=%fused_computation.221 | loop fusion | flops 36172032 | bytes 31500288 | tf_op jit(solution)/shard_map/transpose(jvp())/reduce_sum | solution.py:25
  845.8 9.5 fusion.131
  876.8 11.2 add_add_fusion
  888.6 13.0 fusion.175
  914.0 76.9 %all-reduce.34 = bf16[2048,256]{1,0:T(8,128)(2,1)S(1)} all-reduce(f32[2048,256]{1,0:T(8,128)} %bitcast.538), channel_id=1, replica_groups=mesh['dp'=8,'tensor'=4] {'tensor'}, use_global_device_ids=true, to_apply=%region_22.23 | all-reduce | flops 524288 | bytes 3145728 | tf_op jit(solution)/shard_map/psum | solution.py:210
  998.5 8.9 fusion.189
  1034.2 11.8 all-reduce.29
  1046.0 37.9 %all-reduce.27 = (f32[384]{0:T(512)}, f32[4,768]{1,0:T(4,128)}, f32[768]{0:T(1024)}, f32[4,256]{1,0:T(4,128)}, f32[256]{0:T(256)}, /*index=5*/f32[12]{0:T(128)}, f32[12]{0:T(128)}, f32[12]{0:T(128)}, f32[768]{0:T(1024)}) all-reduce(f32[384]{0:T(512)S(1)} %get-tuple-element.1858, ...), channel_id=1, replica_groups=mesh['dp'=8,'tensor'=4] {'dp'}, use_global_device_ids=true, to_apply=%region_26.27 | all-reduce | flops 6308 | bytes 50464 | tf_op jit(solution)/shard_map/psum | solution.py:251
  1083.9 36.1 %reduce-scatter.3.cloned.1.call-done = f32[2048,384]{1,0:T(8,128)} async-done(((f32[2048,1536]{1,0:T(8,128)}), f32[2048,384]{1,0:T(8,128)}) %reduce-scatter.3.cloned.1.call-update) | async-done | bytes 3145744 | tf_op jit(solution)/shard_map/reduce_scatter | solution.py:187
  1125.7 455.1 %all-reduce.33.cloned.1.call-done = (f32[1536,768]{1,0:T(8,128)}, f32[1536,768]{1,0:T(8,128)}, f32[384,256]{1,0:T(8,128)}, f32[1536,12]{0,1:T(8,128)}, f32[768,1536]{1,0:T(8,128)}) async-done(((f32[1536,768]{1,0:T(8,128)}, f32[1536,768]{1,0:T(8,128)}, f32[384,256]{1,0:T(8,128)}, f32[1536,12]{0,1:T(8,128)}, f32[768,1536]{1,0:T(8,128)}), (f32[1536,768]{1,0:T(8,128)}, f32[1536,768]{1,0:T(8,128)}, ...) | async-done | bytes 14622736 | tf_op jit(solution)/shard_map/psum | solution.py:251
  (651 shorter events, 636.1 us)
Async XLA Ops:
  7.2 411.0 %copy-start = (bf16[1536,768]{1,0:T(8,128)(2,1)S(1)}, bf16[1536,768]{1,0:T(8,128)(2,1)}, u32[]{:S(2)}) copy-start(bf16[1536,768]{1,0:T(8,128)(2,1)} %param.24) | copy-start | bytes 7077892
  7.2 55.7 %copy-start.48 = (f32[1536]{0:T(1024)S(1)}, f32[1536]{0:T(1024)}, u32[]{:S(2)}) copy-start(f32[1536]{0:T(1024)} %param.23) | copy-start | bytes 18436
  7.2 51.4 %all-gather.3.cloned.1.call-start = ((), (), s32[]{:S(2)}) async-start(), calls=%async_computation.2 | async-start | bytes 7864320 | tf_op jit(solution)/shard_map/all_gather | solution.py:158
  7.9 432.1 %all-gather.5.cloned.1.call-start = ((), (), s32[]{:S(2)}) async-start(), calls=%async_computation.4 | async-start | bytes 7864320 | tf_op jit(solution)/shard_map/all_gather | solution.py:189
  8.7 1019.0 %reduce-scatter.5.cloned.1.call-start = ((), (), s32[]{:S(2)}) async-start(), calls=%async_computation.5 | async-start | bytes 15728640 | tf_op jit(solution)/shard_map/reduce_scatter | solution.py:227
  11.0 74.6 %copy-start.22 = (f32[2,1024]{1,0:T(2,128)}, f32[2,1024]{1,0:T(2,128)S(1)}, u32[]{:S(2)}) copy-start(f32[2,1024]{1,0:T(2,128)S(1)} %get-tuple-element.2061) | copy-start | bytes 24580
  11.0 74.5 %copy-start.24 = (f32[2,1024]{1,0:T(2,128)}, f32[2,1024]{1,0:T(2,128)S(1)}, u32[]{:S(2)}) copy-start(f32[2,1024]{1,0:T(2,128)S(1)} %get-tuple-element.2062) | copy-start | bytes 24580
  11.0 74.5 %copy-start.26 = (f32[2,1024]{1,0:T(2,128)}, f32[2,1024]{1,0:T(2,128)S(1)}, u32[]{:S(2)}) copy-start(f32[2,1024]{1,0:T(2,128)S(1)} %get-tuple-element.2063) | copy-start | bytes 24580
  11.8 54.8 %copy-start.49 = (f32[1,256]{1,0:T(1,128)}, f32[1,256]{1,0:T(1,128)S(1)}, u32[]{:S(2)}) copy-start(f32[1,256]{1,0:T(1,128)S(1)} %get-tuple-element.2065) | copy-start | bytes 3076
  11.8 54.8 %copy-start.51 = (f32[1,256]{1,0:T(1,128)}, f32[1,256]{1,0:T(1,128)S(1)}, u32[]{:S(2)}) copy-start(f32[1,256]{1,0:T(1,128)S(1)} %get-tuple-element.2066) | copy-start | bytes 3076
  11.8 54.8 %copy-start.53 = (f32[1,256]{1,0:T(1,128)}, f32[1,256]{1,0:T(1,128)S(1)}, u32[]{:S(2)}) copy-start(f32[1,256]{1,0:T(1,128)S(1)} %get-tuple-element.2067) | copy-start | bytes 3076
  11.8 54.8 %copy-start.55 = (f32[1,256]{1,0:T(1,128)}, f32[1,256]{1,0:T(1,128)S(1)}, u32[]{:S(2)}) copy-start(f32[1,256]{1,0:T(1,128)S(1)} %get-tuple-element.2064) | copy-start | bytes 3076
  12.8 72.8 %copy-start.37 = (f32[768]{0:T(1024)}, f32[768]{0:T(1024)S(1)}, u32[]{:S(2)}) copy-start(f32[768]{0:T(1024)S(1)} %get-tuple-element.1868) | copy-start | bytes 9220
  12.8 72.8 %copy-start.39 = (f32[768]{0:T(1024)}, f32[768]{0:T(1024)S(1)}, u32[]{:S(2)}) copy-start(f32[768]{0:T(1024)S(1)} %get-tuple-element.1869) | copy-start | bytes 9220
  12.8 72.8 %copy-start.41 = (f32[768]{0:T(1024)}, f32[768]{0:T(1024)S(1)}, u32[]{:S(2)}) copy-start(f32[768]{0:T(1024)S(1)} %get-tuple-element.1870) | copy-start | bytes 9220
  12.8 72.8 %copy-start.43 = (f32[768]{0:T(1024)}, f32[768]{0:T(1024)S(1)}, u32[]{:S(2)}) copy-start(f32[768]{0:T(1024)S(1)} %get-tuple-element.1867) | copy-start | bytes 9220
  13.5 107.8 %copy-start.59 = (f32[12]{0:T(128)}, f32[12]{0:T(128)S(1)}, u32[]{:S(2)}) copy-start(f32[12]{0:T(128)S(1)} %exponential_negate_fusion) | copy-start | bytes 148
  418.2 21.8 %copy-start.62 = (f32[768]{0:T(1024)S(1)}, f32[768]{0:T(1024)}, u32[]{:S(2)}) copy-start(f32[768]{0:T(1024)} %param.35) | copy-start | bytes 9220
  440.0 17.4 %copy-start.45 = (f32[2048]{0:T(1024)}, f32[2048]{0:T(1024)S(1)}, u32[]{:S(2)}) copy-start(f32[2048]{0:T(1024)S(1)} %add_rsqrt_fusion) | copy-start | bytes 24580
  500.9 16.4 %copy-start.1 = (f32[1,2,256,12,64]{2,0,1,4,3:T(1,128)}, f32[1,2,256,12,64]{2,0,1,4,3:T(1,128)S(1)}, u32[]{:S(2)}) copy-start(f32[1,2,256,12,64]{2,0,1,4,3:T(1,128)S(1)} %constant_dynamic-slice_fusion.11) | copy-start | bytes 4718596 | tf_op jit(solution)/shard_map/transpose(jvp())/while
  534.9 17.4 %copy-start.21 = (f32[2,256,12]{1,2,0:T(8,128)S(1)}, f32[2,256,12]{1,2,0:T(8,128)}, u32[]{:S(2)}) copy-start(f32[2,256,12]{1,2,0:T(8,128)} %get-tuple-element.2496) | copy-start | bytes 73732 | tf_op jit(solution)/shard_map/transpose(jvp())/while
  575.5 16.4 %copy-start.1 = (f32[1,2,256,12,64]{2,0,1,4,3:T(1,128)}, f32[1,2,256,12,64]{2,0,1,4,3:T(1,128)S(1)}, u32[]{:S(2)}) copy-start(f32[1,2,256,12,64]{2,0,1,4,3:T(1,128)S(1)} %constant_dynamic-slice_fusion.11) | copy-start | bytes 4718596 | tf_op jit(solution)/shard_map/transpose(jvp())/while
  609.4 17.4 %copy-start.21 = (f32[2,256,12]{1,2,0:T(8,128)S(1)}, f32[2,256,12]{1,2,0:T(8,128)}, u32[]{:S(2)}) copy-start(f32[2,256,12]{1,2,0:T(8,128)} %get-tuple-element.2496) | copy-start | bytes 73732 | tf_op jit(solution)/shard_map/transpose(jvp())/while
  650.0 16.4 %copy-start.1 = (f32[1,2,256,12,64]{2,0,1,4,3:T(1,128)}, f32[1,2,256,12,64]{2,0,1,4,3:T(1,128)S(1)}, u32[]{:S(2)}) copy-start(f32[1,2,256,12,64]{2,0,1,4,3:T(1,128)S(1)} %constant_dynamic-slice_fusion.11) | copy-start | bytes 4718596 | tf_op jit(solution)/shard_map/transpose(jvp())/while
  684.0 17.3 %copy-start.21 = (f32[2,256,12]{1,2,0:T(8,128)S(1)}, f32[2,256,12]{1,2,0:T(8,128)}, u32[]{:S(2)}) copy-start(f32[2,256,12]{1,2,0:T(8,128)} %get-tuple-element.2496) | copy-start | bytes 73732 | tf_op jit(solution)/shard_map/transpose(jvp())/while
  758.6 17.4 %copy-start.21 = (f32[2,256,12]{1,2,0:T(8,128)S(1)}, f32[2,256,12]{1,2,0:T(8,128)}, u32[]{:S(2)}) copy-start(f32[2,256,12]{1,2,0:T(8,128)} %get-tuple-element.2496) | copy-start | bytes 73732 | tf_op jit(solution)/shard_map/transpose(jvp())/while
  823.1 17.2 %copy-start.38 = (f32[768]{0:T(1024)S(1)}, f32[768]{0:T(1024)}, u32[]{:S(2)}) copy-start(f32[768]{0:T(1024)} %copy-done.37) | copy-start | bytes 9220
  823.1 17.2 %copy-start.40 = (f32[768]{0:T(1024)S(1)}, f32[768]{0:T(1024)}, u32[]{:S(2)}) copy-start(f32[768]{0:T(1024)} %copy-done.39) | copy-start | bytes 9220
  823.1 17.2 %copy-start.42 = (f32[768]{0:T(1024)S(1)}, f32[768]{0:T(1024)}, u32[]{:S(2)}) copy-start(f32[768]{0:T(1024)} %copy-done.41) | copy-start | bytes 9220
  888.0 232.0 %reduce-scatter.3.cloned.1.call-start = ((), (), s32[]{:S(2)}) async-start(), calls=%async_computation.3 | async-start | bytes 15728640 | tf_op jit(solution)/shard_map/reduce_scatter | solution.py:187
  901.7 679.0 %all-reduce.33.cloned.1.call-start = ((), (), s32[]{:S(2)}) async-start(), calls=%async_computation.6 | async-start | bytes 29294592 | tf_op jit(solution)/shard_map/psum | solution.py:251
  1025.6 20.3 %copy-start.64 = (f32[12]{0:T(128)S(1)}, f32[12]{0:T(128)}, u32[]{:S(2)}) copy-start(f32[12]{0:T(128)} %reduce_sum.391) | copy-start | bytes 148
  (72 other events, 609.1 us)
Sparse Core Ops, SparseCore 0:
  9.6 48.9 all-gather.2
  60.2 46.2 all-gather.4
  888.1 132.1 reduce-scatter.4
  1022.8 97.1 reduce-scatter.2
  1126.2 454.5 all-reduce.32
where the time goes:
time: 1610 us; the launch traced here: 1600 us
  waiting for transfers between devices  536 us (33%)
  matrix products  359 us (22%)
  local copies, waits for them, and re-layouts  287 us (18%)
  other arithmetic  262 us (16%)
  blocking collectives  138 us (9%)
    psum x1, waiting for transfers between devices, local(): lax.psum((prenorm_grad, gating_grad, signal_grad, memory_grad, timestep_g...  455 us
    dot_general x12, matrix products, advance(): jnp.einsum('btsh,bshp->bthp', mixing, piece_signal, precision=highest)  131 us
    dynamic_update_slice x32, other arithmetic, span_scan(): finished, outputs = lax.scan(advance, starting, block_inputs)  85 us
    psum x1, blocking collectives, local(): lax.psum((memory_back, window_grad, shifts_grad), 'tensor')  76.9 us
    dot_general x5, matrix products, contract_cols(): lax.dot_general(left_side, right_side, (((1,), (1,)), ((), ())), preferre...  45.8 us
    dot_general x12, matrix products, advance(): jnp.einsum('bsh,bshp,bsn->bhpn', toward, piece_signal, piece_write, preci...  45.1 us
    all_gather x1, waiting for transfers between devices, local(): gathered = lax.all_gather(tokens, 'tensor', axis=1, tiled=True)  43.8 us
    dynamic_update_slice x36, local copies, waits for them, and re-layouts, span_scan(): finished, outputs = lax.scan(advance, starting, block_inputs)  39.4 us
  transfers between devices with their start and end apart: 5, of which 3 were waited for; matrix products, arithmetic and copies ran while one was open for 28% of the time, Pallas kernels for 0%

commit v1 on v0

v1 whole, which is shorter than its diff:
```python
from functools import partial

import jax
import jax.numpy as jnp
from jax import lax
from jax.experimental import pallas as pl
from jax.experimental.pallas import tpu as pltpu
from jax.sharding import PartitionSpec as P

SEQLEN = 1024
CHUNK = 128
LANES = 128
HALO = 8
LOG2E = 1.4426950408889634
epsilon = 1e-05
f32 = jnp.float32
bf16 = jnp.bfloat16


def dot_nn(a, b):
    return lax.dot_general(a, b, (((1,), (0,)), ((), ())), preferred_element_type=f32)


def dot_nt(a, b):
    return lax.dot_general(a, b, (((1,), (1,)), ((), ())), preferred_element_type=f32)


def dot_tn(a, b):
    return lax.dot_general(a, b, (((0,), (0,)), ((), ())), preferred_element_type=f32)


def halves(v):
    hi = v.astype(bf16)
    lo = (v - hi.astype(f32)).astype(bf16)
    return hi, lo


def spread_heads(v, twice):
    hi, lo = halves(v)
    return dot_nn(jnp.concatenate([hi, lo], axis=1), twice)


def sum_heads(v, once):
    hi, lo = halves(v)
    return dot_nt(hi, once) + dot_nt(lo, once)


def tri_dot(tri, v):
    hi = v.astype(bf16)
    rest = v - hi.astype(f32)
    mid = rest.astype(bf16)
    lo = (rest - mid.astype(f32)).astype(bf16)
    return dot_nn(tri, hi) + (dot_nn(tri, mid) + dot_nn(tri, lo))


def softplus(v):
    return jnp.maximum(v, 0.0) + jnp.log1p(jnp.exp(-jnp.abs(v)))


def precise_nt(a, b):
    ah, al = halves(a)
    bh, bl = halves(b)
    return dot_nt(jnp.concatenate([ah, ah, al], axis=1), jnp.concatenate([bh, bl, bh], axis=1))


def filtered(ext, value, halo, weight, offset, masks):
    rows = value.shape[0]
    ext[0:HALO, :] = halo
    ext[HALO : HALO + rows, :] = value
    out = offset + weight[0:1, :] * value
    moved = []
    for k in range(1, 4):
        shifted = ext[HALO - k : HALO - k + rows, :] * masks[k - 1]
        moved.append(shifted)
        out = out + weight[k : k + 1, :] * shifted
    return out, moved


def filter_back(ext, grad, later, weight, masks):
    rows = grad.shape[0]
    ext[0:rows, :] = grad
    ext[rows : rows + HALO, :] = later
    out = weight[0:1, :] * grad
    for k in range(1, 4):
        out = out + weight[k : k + 1, :] * (ext[k : k + rows, :] * masks[k - 1])
    return out


def block_pair(v):
    lane = lax.broadcasted_iota(jnp.int32, v.shape, 1)
    zero = jnp.zeros_like(v)
    return jnp.concatenate([jnp.where(lane < 64, v, zero), jnp.where(lane < 64, zero, v)], axis=0)


def forward_kernel(
    gate_ref, sig_ref, sigh_ref, mem_ref, memh_ref, step_ref, col_ref, row_ref, back_ref,
    kern_ref, off_ref, win_ref, shf_ref, base_ref, nrate_ref, short_ref, post_ref, ind_ref,
    y_ref, state_ref, stat_ref, held, ext, extm,
):
    rows = CHUNK
    inner = sig_ref.shape[1]
    pairs = inner // LANES

    @pl.when(pl.program_id(1) == 0)
    def _():
        held[...] = jnp.zeros_like(held)

    col = col_ref[...]
    masks = [col[:, k : k + 1] for k in range(3)]
    carried, keep, segc = col[:, 3:4], col[:, 4:5], col[:, 5:6]
    segr = row_ref[0:1, :]
    pre, _ = filtered(ext, sig_ref[...], sigh_ref[...], kern_ref[...], off_ref[...], masks)
    xs = pre * jax.nn.sigmoid(pre)
    prem, _ = filtered(extm, mem_ref[...], memh_ref[...], win_ref[...], shf_ref[...], masks)
    ms = prem * jax.nn.sigmoid(prem)
    writes, reads = ms[:, :LANES], ms[:, LANES:]
    step = softplus(step_ref[...] + base_ref[...])
    rate = nrate_ref[...] * step
    ti = lax.broadcasted_iota(jnp.int32, (rows, rows), 0)
    si = lax.broadcasted_iota(jnp.int32, (rows, rows), 1)
    tri = (si <= ti).astype(f32).astype(bf16)
    cum = tri_dot(tri, rate)
    cum2 = cum * LOG2E
    cum2_rows = cum2.T
    last = cum[rows - 1 : rows, :]
    enter = jnp.exp(cum) * carried
    toward = jnp.exp(last - cum) * keep
    once = ind_ref[0:LANES, :]
    twice = ind_ref[...]
    step_e = spread_heads(step, twice)
    enter_e = spread_heads(enter, twice)
    toward_e = spread_heads(toward, twice)
    scores = precise_nt(reads, writes)
    scores = jnp.where((si <= ti) & (segc == segr), scores, 0.0)
    u = step_e * xs
    ub = u.astype(bf16)
    state = held[...]
    state_ref[...] = state
    inter = dot_nn(reads.astype(bf16), state.astype(bf16))
    outs = []
    for j in range(pairs):
        parts = []
        for h in (2 * j, 2 * j + 1):
            fall = jnp.exp2(jnp.minimum(cum2[:, h : h + 1] - cum2_rows[h : h + 1, :], 0.0))
            parts.append((fall * scores).astype(bf16))
        upair = block_pair(ub[:, j * LANES : (j + 1) * LANES])
        outs.append(dot_nn(jnp.concatenate(parts, axis=1), upair))
    y = jnp.concatenate(outs, axis=1) + inter * enter_e + short_ref[...] * xs
    y_ref[...] = y
    held[...] = state * enter_e[rows - 1 : rows, :] + dot_nn(
        writes.T.astype(bf16), (toward_e * u).astype(bf16)
    )
    gate = gate_ref[...]
    gated = y * (gate * jax.nn.sigmoid(gate))
    squares = jnp.sum(gated * gated, axis=1, keepdims=True)
    dots = jnp.sum(gated * (back_ref[...] * post_ref[...]), axis=1, keepdims=True)
    lane = lax.broadcasted_iota(jnp.int32, (rows, LANES), 1)
    both = jnp.where(lane == 0, squares, jnp.where(lane == 1, dots, 0.0))
    stat_ref[...] = both.T[0:8, :]


def backward_kernel(
    gate_ref, sig_ref, sigh_ref, mem_ref, memh_ref, step_ref, col_ref, row_ref, back_ref,
    y_ref, fac_ref, state_ref,
    kern_ref, off_ref, win_ref, shf_ref, base_ref, nrate_ref, short_ref, post_ref, ind_ref,
    dgate_ref, dsig_ref, dmem_ref, dstep_ref, wide_ref, window_ref, head_ref,
    held, ext, extm, later, laterm,
):
    rows = CHUNK
    inner = sig_ref.shape[1]
    pairs = inner // LANES
    inv_inner = fac_ref[:, 2:3]

    @pl.when(pl.program_id(1) == 0)
    def _():
        held[...] = jnp.zeros_like(held)
        later[...] = jnp.zeros_like(later)
        laterm[...] = jnp.zeros_like(laterm)

    @pl.when((pl.program_id(0) == 0) & (pl.program_id(1) == 0))
    def _():
        wide_ref[...] = jnp.zeros_like(wide_ref)
        window_ref[...] = jnp.zeros_like(window_ref)
        head_ref[...] = jnp.zeros_like(head_ref)

    col = col_ref[...]
    masks = [col[:, k : k + 1] for k in range(3)]
    carried, keep, segc = col[:, 3:4], col[:, 4:5], col[:, 5:6]
    ahead = [col[:, k : k + 1] for k in range(6, 9)]
    segr = row_ref[0:1, :]

    factor = fac_ref[:, 0:1]
    gate = gate_ref[...]
    y = y_ref[...]
    back = back_ref[...]
    sg = jax.nn.sigmoid(gate)
    sl = gate * sg
    balanced = y * sl * factor
    grad = factor * (back * post_ref[...] - balanced * inv_inner)
    wide_ref[5:6, :] += jnp.sum(back * balanced, axis=0, keepdims=True)
    dy = grad * sl
    dgate_ref[...] = (grad * y * (sg * (1.0 + gate * (1.0 - sg)))).astype(bf16)

    kern = kern_ref[...]
    win = win_ref[...]
    pre, moved = filtered(ext, sig_ref[...], sigh_ref[...], kern, off_ref[...], masks)
    sp = jax.nn.sigmoid(pre)
    xs = pre * sp
    prem, movedm = filtered(extm, mem_ref[...], memh_ref[...], win, shf_ref[...], masks)
    spm = jax.nn.sigmoid(prem)
    ms = prem * spm
    writes, reads = ms[:, :LANES], ms[:, LANES:]
    shifted = step_ref[...] + base_ref[...]
    step = softplus(shifted)
    nrate = nrate_ref[...]
    rate = nrate * step
    si = lax.broadcasted_iota(jnp.int32, (rows, rows), 0)
    ti = lax.broadcasted_iota(jnp.int32, (rows, rows), 1)
    low = (ti <= si).astype(f32).astype(bf16)
    low_strict = (ti < si).astype(f32).astype(bf16)
    high = (ti >= si).astype(f32).astype(bf16)
    cum = tri_dot(low, rate)
    cum2 = cum * LOG2E
    cum2_rows = cum2.T
    last = cum[rows - 1 : rows, :]
    enter = jnp.exp(cum) * carried
    toward = jnp.exp(last - cum) * keep
    once = ind_ref[0:LANES, :]
    twice = ind_ref[...]
    step_e = spread_heads(step, twice)
    enter_e = spread_heads(enter, twice)
    toward_e = spread_heads(toward, twice)
    seg_row = segr
    inside = (si <= ti) & (segc == seg_row)
    scores = precise_nt(writes, reads)
    scores_in = jnp.where(inside, scores, 0.0)
    scores_strict = jnp.where(inside & (si < ti), scores, 0.0)
    u = step_e * xs
    ub = u.astype(bf16)
    dyb = dy.astype(bf16)
    state = state_ref[...]
    dstate = held[...]
    stateb = state.astype(bf16)
    dstateb = dstate.astype(bf16)
    rb = reads.astype(bf16)
    wb = writes.astype(bf16)

    dscore = jnp.zeros((rows, rows), f32)
    lane = lax.broadcasted_iota(jnp.int32, (rows, LANES), 1)
    as_source = jnp.zeros((rows, LANES), f32)
    as_target = []
    dus = []
    for j in range(pairs):
        dypair = block_pair(dyb[:, j * LANES : (j + 1) * LANES])
        cross = dot_nt(ub[:, j * LANES : (j + 1) * LANES], dypair)
        parts = []
        for i, h in enumerate((2 * j, 2 * j + 1)):
            fall = jnp.exp2(jnp.minimum(cum2_rows[h : h + 1, :] - cum2[:, h : h + 1], 0.0))
            parts.append((fall * scores_in).astype(bf16))
            weighted = fall * cross[:, i * rows : (i + 1) * rows]
            dscore = dscore + weighted
            flow = weighted * scores_strict
            as_source = jnp.where(lane == h, jnp.sum(flow, axis=1, keepdims=True), as_source)
            as_target.append(jnp.sum(flow, axis=0, keepdims=True))
        dus.append(dot_nn(jnp.concatenate(parts, axis=1), dypair))
    target = jnp.concatenate(
        as_target + [jnp.zeros((LANES - 2 * pairs, rows), f32)], axis=0
    ).T
    dscore = jnp.where(inside, dscore, 0.0)

    leaving = toward_e * dot_nn(wb, dstateb)
    du = jnp.concatenate(dus, axis=1) + leaving
    entered = enter_e * dy
    arriving = entered * dot_nn(rb, stateb)
    dx = short_ref[...] * dy + step_e * du
    dscore_b = dscore.astype(bf16)
    dwrites = dot_nn(dscore_b, rb) + dot_nt((toward_e * u).astype(bf16), dstateb)
    enteredb = entered.astype(bf16)
    dreads = dot_nn(dscore.T.astype(bf16), wb) + dot_nt(enteredb, stateb)
    persist_e = enter_e[rows - 1 : rows, :]
    across = jnp.sum(dstate * state, axis=0, keepdims=True) * persist_e
    held[...] = dstate * persist_e + dot_nn(reads.T.astype(bf16), enteredb)

    dstep_direct = sum_heads(xs * du, once)
    sent = sum_heads(u * leaving, once)
    got = sum_heads(arriving, once)
    across_h = sum_heads(jnp.broadcast_to(across, (8, inner)), once)[0:1, :]
    drate = tri_dot(high, got + target - as_source) + tri_dot(low_strict, sent) + across_h
    dstep = (nrate * drate + dstep_direct) * jax.nn.sigmoid(shifted)
    dstep_ref[...] = dstep.astype(bf16)
    head_ref[0:1, :] += jnp.sum(dstep, axis=0, keepdims=True)
    head_ref[1:2, :] += jnp.sum(drate * rate, axis=0, keepdims=True)
    wide_ref[6:7, :] += jnp.sum(dy * xs, axis=0, keepdims=True)

    dpre = dx * (sp * (1.0 + pre * (1.0 - sp)))
    dsig_ref[...] = filter_back(ext, dpre, later[...], kern, ahead).astype(bf16)
    later[...] = dpre[0:HALO, :]
    wide_ref[0:1, :] += jnp.sum(dpre * sig_ref[...], axis=0, keepdims=True)
    for k in range(3):
        wide_ref[k + 1 : k + 2, :] += jnp.sum(dpre * moved[k], axis=0, keepdims=True)
    wide_ref[4:5, :] += jnp.sum(dpre, axis=0, keepdims=True)
    dprem = jnp.concatenate([dwrites, dreads], axis=1) * (spm * (1.0 + prem * (1.0 - spm)))
    dmem_ref[...] = filter_back(extm, dprem, laterm[...], win, ahead).astype(bf16)
    laterm[...] = dprem[0:HALO, :]
    window_ref[0:1, :] += jnp.sum(dprem * mem_ref[...], axis=0, keepdims=True)
    for k in range(3):
        window_ref[k + 1 : k + 2, :] += jnp.sum(dprem * movedm[k], axis=0, keepdims=True)
    window_ref[4:5, :] += jnp.sum(dprem, axis=0, keepdims=True)


def full_spec(shape):
    return pl.BlockSpec(shape, lambda b, c: (0,) * len(shape))


def mixer_columns(segments):
    rows = segments.reshape(-1, SEQLEN)
    place = jnp.arange(SEQLEN, dtype=jnp.int32)[None, :]
    out = []
    for k in range(1, 4):
        earlier = jnp.roll(rows, k, axis=1)
        out.append((earlier == rows) & (place >= k))
    chunked = rows.reshape(rows.shape[0], SEQLEN // CHUNK, CHUNK)
    tail = chunked[:, :, -1]
    before = jnp.concatenate([jnp.full_like(tail[:, :1], -1), tail[:, :-1]], axis=1)
    out.append((chunked == before[:, :, None]).reshape(rows.shape))
    out.append((chunked == tail[:, :, None]).reshape(rows.shape))
    out.append(rows)
    for k in range(1, 4):
        ahead = jnp.roll(rows, -k, axis=1)
        out.append((ahead == rows) & (place < SEQLEN - k))
    cols = jnp.stack([member.reshape(-1).astype(f32) for member in out], axis=1)
    cols = jnp.pad(cols, ((0, 0), (0, 16 - cols.shape[1])))
    row = jnp.broadcast_to(segments.astype(f32)[None, :], (8, segments.shape[0]))
    return cols, row


def specs(inner, reverse):
    chunks = SEQLEN // CHUNK
    step = CHUNK // HALO

    def at(b, c):
        return b * chunks + (chunks - 1 - c if reverse else c)

    def tall(width):
        return pl.BlockSpec((CHUNK, width), lambda b, c: (at(b, c), 0))

    def halo(width):
        return pl.BlockSpec((HALO, width), lambda b, c: (jnp.maximum(at(b, c) * step - 1, 0), 0))

    flat = pl.BlockSpec((8, CHUNK), lambda b, c: (0, at(b, c)))
    data = [tall(inner), tall(inner), halo(inner), tall(2 * LANES), halo(2 * LANES), tall(LANES), tall(16), flat, tall(inner)]
    weights = [full_spec((4, inner)), full_spec((1, inner)), full_spec((4, 2 * LANES)), full_spec((1, 2 * LANES)), full_spec((1, LANES)), full_spec((1, LANES)), full_spec((1, inner)), full_spec((1, inner)), full_spec((2 * LANES, inner))]
    return tall, flat, data, weights


def mixer_forward(data, weights):
    tokens, inner = data[0].shape
    chunks = SEQLEN // CHUNK
    tall, flat, dspecs, wspecs = specs(inner, False)
    return pl.pallas_call(
        forward_kernel,
        grid=(tokens // SEQLEN, chunks),
        in_specs=dspecs + wspecs,
        out_specs=[tall(inner), tall(inner), flat],
        out_shape=[
            jax.ShapeDtypeStruct((tokens, inner), f32),
            jax.ShapeDtypeStruct((tokens, inner), f32),
            jax.ShapeDtypeStruct((8, tokens), f32),
        ],
        scratch_shapes=[
            pltpu.VMEM((LANES, inner), f32),
            pltpu.VMEM((CHUNK + HALO, inner), f32),
            pltpu.VMEM((CHUNK + HALO, 2 * LANES), f32),
        ],
        compiler_params=pltpu.CompilerParams(dimension_semantics=("arbitrary", "arbitrary"), vmem_limit_bytes=50 << 20),
        name="mixer_forward",
    )(*data, *weights)


def mixer_backward(data, y, fac, states, weights):
    tokens, inner = data[0].shape
    chunks = SEQLEN // CHUNK
    tall, flat, dspecs, wspecs = specs(inner, True)
    return pl.pallas_call(
        backward_kernel,
        grid=(tokens // SEQLEN, chunks),
        in_specs=dspecs + [tall(inner), tall(fac.shape[1]), tall(inner)] + wspecs,
        out_specs=[tall(inner), tall(inner), tall(2 * LANES), tall(LANES), full_spec((8, inner)), full_spec((8, 2 * LANES)), full_spec((8, LANES))],
        out_shape=[
            jax.ShapeDtypeStruct((tokens, inner), bf16),
            jax.ShapeDtypeStruct((tokens, inner), bf16),
            jax.ShapeDtypeStruct((tokens, 2 * LANES), bf16),
            jax.ShapeDtypeStruct((tokens, LANES), bf16),
            jax.ShapeDtypeStruct((8, inner), f32),
            jax.ShapeDtypeStruct((8, 2 * LANES), f32),
            jax.ShapeDtypeStruct((8, LANES), f32),
        ],
        scratch_shapes=[
            pltpu.VMEM((LANES, inner), f32),
            pltpu.VMEM((CHUNK + HALO, inner), f32),
            pltpu.VMEM((CHUNK + HALO, 2 * LANES), f32),
            pltpu.VMEM((HALO, inner), f32),
            pltpu.VMEM((HALO, 2 * LANES), f32),
        ],
        compiler_params=pltpu.CompilerParams(dimension_semantics=("arbitrary", "arbitrary"), vmem_limit_bytes=50 << 20),
        name="mixer_backward",
    )(*data, y, fac, states, *weights)


def contract_rows(left_side, right_side):
    return lax.dot_general(left_side, right_side, (((0,), (0,)), ((), ())), preferred_element_type=f32)


def local(
    tokens, segments, prenorm, gating, signal, memory, timestep, kernel, offsets, window, shifts,
    baseline, decays, shortcut, postnorm, readout, cotangent,
):
    width_here = tokens.shape[1]
    width = memory.shape[0]
    groups = width // width_here
    inner = gating.shape[1]
    whole = inner * groups
    heads = baseline.shape[0]
    position = lax.axis_index("tensor") * width_here
    gain_here = lax.dynamic_slice_in_dim(prenorm, position, width_here)
    tokens_wide = tokens.astype(f32)
    gathered = lax.all_gather(tokens, "tensor", axis=1, tiled=True)
    piece = lax.all_gather(cotangent, "tensor", axis=1, tiled=True)
    gathered_wide = gathered.astype(f32)
    inverse = lax.rsqrt(jnp.mean(gathered_wide * gathered_wide, axis=-1, keepdims=True) + epsilon)
    normed = (gathered_wide * inverse * prenorm).astype(bf16)
    scaled_rows = tokens_wide * inverse
    timestep_wide = jnp.pad(timestep, ((0, 0), (0, LANES - heads)))
    gate_in = jnp.dot(normed, gating, preferred_element_type=f32)
    signal_in = jnp.dot(normed, signal, preferred_element_type=f32)
    memory_in = jnp.dot(normed, memory, preferred_element_type=f32)
    step_in = jnp.dot(normed, timestep_wide, preferred_element_type=f32)
    back_rows = dot_nt(piece, readout)

    cols, row = mixer_columns(segments)
    head_width = inner // heads
    once = jnp.repeat(jnp.eye(LANES, heads, dtype=f32), head_width, axis=1).astype(bf16)
    pad = lambda v: jnp.pad(v[None, :], ((0, 0), (0, LANES - heads)))
    weights = (
        kernel, offsets[None, :], window, shifts[None, :], pad(baseline), pad(-jnp.exp(decays)),
        jnp.repeat(shortcut, head_width)[None, :], postnorm[None, :], jnp.concatenate([once, once], axis=0),
    )
    data = (gate_in, signal_in, signal_in, memory_in, memory_in, step_in, cols, row, back_rows)
    y, states, stat = mixer_forward(data, weights)
    sums = lax.psum(stat[0:2], "tensor")
    factor = lax.rsqrt(sums[0] / whole + epsilon)
    dots = sums[1] * factor
    fac = jnp.stack([factor, dots, dots / whole], axis=1)
    outnormed = (y * (gate_in * jax.nn.sigmoid(gate_in)) * factor[:, None] * postnorm).astype(bf16)
    readout_grad = contract_rows(outnormed, piece)
    readout_grad = lax.psum(readout_grad.astype(bf16), "dp")
    partial_out = jnp.dot(outnormed, readout, preferred_element_type=f32).astype(bf16)
    summed_out = lax.psum_scatter(partial_out, "tensor", scatter_dimension=1, tiled=True)
    outcome = (tokens_wide + summed_out.astype(f32)).astype(bf16)

    gate_low, signal_low, memory_low, step_low, wide, window_sums, head_sums = mixer_backward(
        data, y, fac, states, weights
    )
    gating_grad = contract_rows(normed, gate_low)
    gating_grad = lax.psum(gating_grad.astype(bf16), "dp")
    signal_grad = contract_rows(normed, signal_low)
    signal_grad = lax.psum(signal_grad.astype(bf16), "dp")
    normed_part = (
        dot_nt(gate_low, gating) + dot_nt(signal_low, signal)
        + dot_nt(step_low, timestep_wide) + dot_nt(memory_low, memory)
    )
    scaled_all = gathered_wide * inverse
    norm_dots = lax.psum(jnp.sum(normed_part * prenorm * scaled_all, axis=-1), "tensor")
    normed_back = lax.psum_scatter(normed_part.astype(bf16), "tensor", scatter_dimension=1, tiled=True).astype(f32)
    scaled_back = normed_back * gain_here
    prenorm_grad = jnp.sum(normed_back * scaled_rows, axis=0)
    tokens_grad = inverse * (scaled_back - scaled_rows * norm_dots[:, None] / width) + cotangent.astype(f32)

    timestep_grad = contract_rows(normed, step_low)[:, :heads]
    memory_grad = contract_rows(normed, memory_low)
    memory_grad = lax.psum_scatter(memory_grad, "tensor", scatter_dimension=0, tiled=True)
    window_sums = lax.psum(window_sums, ("dp", "tensor"))
    shortcut_grad = wide[6].reshape(heads, head_width).sum(axis=1)
    prenorm_grad, memory_grad, timestep_grad, wide, head_sums, shortcut_grad = lax.psum(
        (prenorm_grad, memory_grad, timestep_grad, wide[:6], head_sums[:2, :heads], shortcut_grad), "dp"
    )
    return (
        outcome, tokens_grad, prenorm_grad, gating_grad.astype(f32), signal_grad.astype(f32), memory_grad,
        timestep_grad, wide[0:4], wide[4], window_sums[0:4], window_sums[4], head_sums[0], head_sums[1],
        shortcut_grad, wide[5], readout_grad.astype(f32),
    )


def solution(mesh):
    placed = (
        P("dp", "tensor"), P("dp"), P(), P(None, "tensor"), P(None, "tensor"), P(), P(None, "tensor"),
        P(None, "tensor"), P("tensor"), P(), P(), P("tensor"), P("tensor"), P("tensor"), P("tensor"),
        P("tensor", None), P("dp", "tensor"),
    )
    return jax.shard_map(
        local,
        mesh=mesh,
        in_specs=placed,
        out_specs=(
            P("dp", "tensor"), P("dp", "tensor"), P("tensor"), P(None, "tensor"), P(None, "tensor"),
            P("tensor", None), P(None, "tensor"), P(None, "tensor"), P("tensor"), P(), P(), P("tensor"),
            P("tensor"), P("tensor"), P("tensor"), P("tensor", None),
        ),
        check_vma=False,
    )
```

time: 1610 us -> 704 us (0.44)
  local copies, waits for them, and re-layouts: 287 us -> 35.4 us
  matrix products: 359 us -> 118 us
  other arithmetic: 262 us -> 30 us
  waiting for transfers between devices: 536 us -> 319 us
  Pallas kernels: 0 us -> 81 us
  blocking collectives: 138 us -> 97.3 us
    psum x1 -> x2, waiting for transfers between devices: 455 us -> 147 us  [the longest x1 117 us: local(): gating_grad = lax.psum(gating_grad.astype(bf16), 'dp')]
    dot_general x58 -> x10, matrix products: 329 us -> 80.9 us  [the longest x5 52.1 us: dot_nt(): lax.dot_general(a, b, (((1,), (1,)), ((), ())), preferred_element_type=f32)]
    unnamed x5 -> x9, waiting for transfers between devices: 1.43 us -> 109 us
    dynamic_update_slice x32 -> x0, other arithmetic: 85 us -> none  [span_scan(): finished, outputs = lax.scan(advance, starting, block_inputs)]
    pallas_call x0 -> x2, Pallas kernels: none -> 81 us  [the longest x1 57.2 us: mixer_backward(): pl.pallas_call(backward_kernel, grid=(tokens // SEQLEN, chunks), in_specs...]
    reduce_sum x17 -> x2, other arithmetic: 68.2 us -> 5.12 us  [the longest x1 5 us: local(): prenorm_grad = jnp.sum(normed_back * scaled_rows, axis=0)]
    reshape x11 -> x1, local copies, waits for them, and re-layouts: 53.7 us -> 0.01 us  [mixer_columns(): rows = segments.reshape(-1, SEQLEN)]
    mul x36 -> x0, local copies, waits for them, and re-layouts: 49 us -> none  [the longest x8 10.1 us: advance(): entering = jnp.exp(running) * carried[:, :, None]]
  transfers between devices with their start and end apart: 5 -> 7, of which waited for: 3 -> 6; matrix products, arithmetic and copies ran while one was open for 28% -> 22% of each run, Pallas kernels for 0% -> 0%
where the time goes in v1:
time: 704 us; the launch traced here: 696 us
  waiting for transfers between devices  319 us (45%)
  matrix products  118 us (17%)
  blocking collectives  97.3 us (14%)
  Pallas kernels  81 us (12%)
  local copies, waits for them, and re-layouts  35.4 us (5%)
  other arithmetic  30 us (4%)
  between operations  14.8 us (2%)
    psum x1, waiting for transfers between devices, local(): gating_grad = lax.psum(gating_grad.astype(bf16), 'dp')  117 us
    unnamed x9, waiting for transfers between devices  109 us
    pallas_call x1, Pallas kernels, mixer_backward(): pl.pallas_call(backward_kernel, grid=(tokens // SEQLEN, chunks), in_specs...  57.2 us
    dot_general x5, matrix products, dot_nt(): lax.dot_general(a, b, (((1,), (1,)), ((), ())), preferred_element_type=f32)  52.1 us
    psum x1, blocking collectives, local(): window_sums = lax.psum(window_sums, ('dp', 'tensor'))  42.5 us
    all_gather x1, waiting for transfers between devices, local(): gathered = lax.all_gather(tokens, 'tensor', axis=1, tiled=True)  40.5 us
    dot_general x5, matrix products, contract_rows(): lax.dot_general(left_side, right_side, (((0,), (0,)), ((), ())), preferre...  37.4 us
    psum x1, blocking collectives, local(): lax.psum((prenorm_grad, memory_grad, timestep_grad, wide[:6], head_sums[:...  37.3 us
  transfers between devices with their start and end apart: 7, of which 6 were waited for; matrix products, arithmetic and copies ran while one was open for 22% of the time, Pallas kernels for 0%

profile of v1, /device:TPU:0, one launch (start us, length us, event | category | flops | bytes accessed | tf_op | source)
XLA Modules:
  0.0 696.3 jit_solution(7708258276687736518)
XLA Ops:
  18.8 40.5 %all-gather.3.cloned.1.call-done = bf16[2048,1536]{0,1:T(8,128)(2,1)} async-done(((bf16[2048,384]{0,1:T(8,128)(2,1)}), bf16[2048,1536]{0,1:T(8,128)(2,1)}) %all-gather.3.cloned.1.call-update) | async-done | bytes 6291472 | tf_op jit(solution)/shard_map/all_gather | solution.py:427
  59.3 4.3 fusion.4
  67.3 3.3 fusion.47.mem_ref.memh_ref
  70.7 7.4 %fusion.45.gate_ref = f32[2048,768]{1,0:T(8,128)} fusion(bf16[2048,1536]{0,1:T(8,128)(2,1)S(1)} %fusion.2, bf16[1536,768]{1,0:T(8,128)(2,1)S(1)} %copy-done.33), kind=kOutput, calls=%fused_computation.91 | convolution fusion | flops 4831838208 | bytes 14942208 | tf_op jit(solution)/shard_map/dot_general | solution.py:434
  78.0 7.2 %fusion.46.sig_ref.sigh_ref = f32[2048,768]{1,0:T(8,128)} fusion(bf16[2048,1536]{0,1:T(8,128)(2,1)S(1)} %fusion.2, bf16[1536,768]{1,0:T(8,128)(2,1)S(1)} %copy-done.31), kind=kOutput, calls=%fused_computation.92 | convolution fusion | flops 4831838208 | bytes 14942208 | tf_op jit(solution)/shard_map/dot_general | solution.py:435
  85.3 21.9 %all-gather.5.cloned.1.call-done = bf16[2048,1536]{1,0:T(8,128)(2,1)} async-done(((bf16[2048,384]{1,0:T(8,128)(2,1)}), bf16[2048,1536]{1,0:T(8,128)(2,1)}) %all-gather.5.cloned.1.call-update) | async-done | bytes 6291472 | tf_op jit(solution)/shard_map/all_gather | solution.py:428
  107.2 9.8 %fusion.48.back_ref = f32[2048,768]{1,0:T(8,128)} fusion(bf16[2048,1536]{1,0:T(8,128)(2,1)} %all-gather.5.cloned.1.call-done, bf16[768,1536]{1,0:T(8,128)(2,1)S(1)} %copy-done), kind=kOutput, calls=%fused_computation.94 | convolution fusion | flops 4831838208 | bytes 14942208 | tf_op jit(solution)/shard_map/dot_general | solution.py:25
  117.1 23.8 %mixer_forward.1 = (f32[2048,768]{1,0:T(8,128)}, f32[2048,768]{1,0:T(8,128)}, f32[8,2048]{1,0:T(8,128)S(1)}) custom-call(f32[2048,768]{1,0:T(8,128)} %fusion.45.gate_ref, f32[2048,768]{1,0:T(8,128)} %fusion.46.sig_ref.sigh_ref, f32[2048,768]{1,0:T(8,128)} %fusion.46.sig_ref.sigh_ref, f32[2048,256]{1,0:T(8,128)} %fusion.47.mem_ref.memh_ref, ...), custom_call_target="tpu_custom_call" | custom-call | tf_op jit(solution)/shard_map/mixer_forward/pallas_call | solution.py:360
  141.4 10.8 %psum.84 = f32[2,2048]{1,0:T(2,128)S(1)} all-reduce(f32[2,2048]{1,0:T(2,128)} %slice.110), channel_id=1, replica_groups=mesh['dp'=8,'tensor'=4] {'tensor'}, use_global_device_ids=true, to_apply=%region_1.2 | all-reduce | flops 4096 | bytes 32768 | tf_op jit(solution)/shard_map/psum | solution.py:450
  156.1 57.2 %mixer_backward.1 = (bf16[2048,768]{1,0:T(8,128)(2,1)}, bf16[2048,768]{1,0:T(8,128)(2,1)}, bf16[2048,256]{1,0:T(8,128)(2,1)S(1)}, bf16[2048,128]{1,0:T(8,128)(2,...) custom-call(f32[2048,768]{1,0:T(8,128)} %fusion.45.gate_ref, ...), custom_call_target="tpu_custom_call" | custom-call | tf_op jit(solution)/shard_map/mixer_backward/pallas_call | solution.py:384
  215.0 5.7 fusion.51
  220.8 9.5 %convolution_convert_fusion.3 = bf16[1536,768]{1,0:T(8,128)(2,1)} fusion(bf16[2048,1536]{0,1:T(8,128)(2,1)} %copy-done.10, bf16[2048,768]{1,0:T(8,128)(2,1)} %get-tuple-element.29), kind=kOutput, calls=%fused_computation.18 | convolution fusion | flops 4833017856 | bytes 11796480 | tf_op jit(solution)/shard_map/dot_general | solution.py:411
  230.3 5.9 multiply_convert_fusion
  236.3 10.5 %convolution_convert_fusion.2 = bf16[1536,768]{1,0:T(8,128)(2,1)} fusion(bf16[2048,1536]{0,1:T(8,128)(2,1)} %copy-done.10, bf16[2048,768]{1,0:T(8,128)(2,1)S(1)} %copy-done.29), kind=kOutput, calls=%fused_computation.17 | convolution fusion | flops 4833017856 | bytes 11796480 | tf_op jit(solution)/shard_map/dot_general | solution.py:411
  246.8 6.5 convolution_convert_fusion.1
  253.4 8.9 %convolution_convert_fusion = bf16[2048,1536]{1,0:T(8,128)(2,1)} fusion(bf16[2048,768]{1,0:T(8,128)(2,1)} %copy-done.12, bf16[768,1536]{1,0:T(8,128)(2,1)S(1)} %copy-done), kind=kOutput, calls=%fused_computation.8 | convolution fusion | flops 4834983936 | bytes 11796480 | tf_op jit(solution)/shard_map/dot_general | solution.py:457
  262.4 8.7 %copy.79 = bf16[2048,1536]{0,1:T(8,128)(2,1)} copy(bf16[2048,1536]{1,0:T(8,128)(2,1)} %convolution_convert_fusion) | data formatting | bytes 12582912
  272.1 6.4 fusion.14
  278.5 8.2 %fusion.50 = f32[2048,1536]{0,1:T(8,128)} fusion(bf16[2048,768]{1,0:T(8,128)(2,1)S(1)} %copy-done.30, bf16[1536,768]{1,0:T(8,128)(2,1)S(1)} %copy-done.32), kind=kOutput, calls=%fused_computation.96 | convolution fusion | flops 4831838208 | bytes 18087936 | tf_op jit(solution)/shard_map/dot_general | solution.py:25
  286.7 7.9 %fusion.49 = f32[2048,1536]{0,1:T(8,128)} fusion(bf16[2048,768]{1,0:T(8,128)(2,1)S(1)} %copy-done.28, bf16[1536,768]{1,0:T(8,128)(2,1)S(1)} %copy-done.34), kind=kOutput, calls=%fused_computation.95 | convolution fusion | flops 4831838208 | bytes 18087936 | tf_op jit(solution)/shard_map/dot_general | solution.py:25
  294.6 19.8 %fusion.3 = (f32[2048]{0:T(1024)S(1)}, bf16[1536,2048]{1,0:T(8,128)(2,1)}) fusion(bf16[2048,1536]{0,1:T(8,128)(2,1)} %all-gather.3.cloned.1.call-done, f32[1536]{0:T(1024)S(1)} %copy-done.24, f32[2048]{0:T(1024)S(1)} %copy-done.19, bf16[2048,256]{1,0:T(8,128)(2,1)} %copy-done.6, bf16[1536,256]{1,0:T(8,128)(2,1)} %param.22, f32[2048,1536]{0,1:T(8,128)} %fusion.14, ...), kind=kOutput, calls=%fused_computation.5 | convolution fusion | flops 1638922240 | bytes 52189184 | tf_op jit(solution)/shard_map/dot_general | solution.py:25
  314.6 42.5 %psum.92 = f32[8,256]{1,0:T(8,128)S(1)} all-reduce(f32[8,256]{1,0:T(8,128)S(1)} %get-tuple-element.34), channel_id=1, replica_groups=mesh['dp'=8,'tensor'=4] {'dp','tensor'}, use_global_device_ids=true, to_apply=%region_14.15 | all-reduce | flops 2048 | bytes 16384 | tf_op jit(solution)/shard_map/psum | solution.py:482
  358.5 6.6 psum.85
  365.1 5.2 fusion.12
  370.3 117.4 %all-reduce.13.cloned.1.call-done = (bf16[1536,768]{1,0:T(8,128)(2,1)}, bf16[1536,768]{1,0:T(8,128)(2,1)}, bf16[768,1536]{1,0:T(8,128)(2,1)}) async-done(((bf16[1536,768]{1,0:T(8,128)(2,1)}, bf16[1536,768]{1,0:T(8,128)(2,1)}, bf16[768,1536]{1,0:T(8,128)(2,1)}), (bf16[1536,768]{1,0:T(8,128)(2,1)}, bf16[1536,768]{1,0:T(8,128)(2,1)}, bf16[768,1536]{1,0:T(8,128)(2,1)})) %all-reduce.13.cloned.1.call-update) | async-done | bytes 7077904 | tf_op jit(solution)/shard_map/psum | solution.py:465
  487.7 4.4 convert_element_type.98
  492.1 3.1 convert_element_type.100
  498.1 50.0 %reduce-scatter.10.cloned.1.call-done = bf16[384,2048]{1,0:T(8,128)(2,1)} async-done(((bf16[1536,2048]{1,0:T(8,128)(2,1)}), bf16[384,2048]{1,0:T(8,128)(2,1)}) %reduce-scatter.10.cloned.1.call-update) | async-done | bytes 1572880
  550.6 58.7 %reduce-scatter.12.cloned.1.call-done = bf16[384,2048]{1,0:T(8,128)(2,1)} async-done(((bf16[1536,2048]{1,0:T(8,128)(2,1)}), bf16[384,2048]{1,0:T(8,128)(2,1)}) %reduce-scatter.12.cloned.1.call-update) | async-done | bytes 1572880
  611.9 5.0 fusion.11
  616.9 37.3 %all-reduce.5 = (f32[384]{0:T(512)}, f32[6,768]{1,0:T(8,128)S(1)}, f32[2,12]{1,0:T(2,128)S(1)}, f32[12]{0:T(128)}) all-reduce(f32[384]{0:T(512)S(1)} %get-tuple-element.52, f32[6,768]{1,0:T(8,128)S(1)} %bitcast.119, f32[2,12]{1,0:T(2,128)S(1)} %slice.119, f32[12]{0:T(128)S(1)} %reduce_sum.39), channel_id=1, replica_groups=mesh['dp'=8,'tensor'=4] {'dp'}, use_global_device_ids=true, to_apply=%region_7.8 | all-reduce | flops 5028 | bytes 40224 | tf_op jit(solution)/shard_map/psum | solution.py:484
  656.0 30.0 %all-reduce.11.cloned.1.call-done = (f32[384,256]{1,0:T(8,128)}, f32[1536,12]{0,1:T(8,128)}) async-done(((f32[384,256]{1,0:T(8,128)}, f32[1536,12]{0,1:T(8,128)}), (f32[384,256]{1,0:T(8,128)}, f32[1536,12]{0,1:T(8,128)})) %all-reduce.11.cloned.1.call-update) | async-done | bytes 466960 | tf_op jit(solution)/shard_map/psum | solution.py:484
  (164 shorter events, 37.0 us)
Async XLA Ops:
  7.2 100.0 %copy-start = (bf16[768,1536]{1,0:T(8,128)(2,1)S(1)}, bf16[768,1536]{1,0:T(8,128)(2,1)}, u32[]{:S(2)}) copy-start(bf16[768,1536]{1,0:T(8,128)(2,1)} %param.32) | copy-start | bytes 7077892
  7.2 3.7 copy-start.26
  7.2 3.7 copy-start.25
  7.2 4.0 copy-start.27
  7.3 52.1 %all-gather.3.cloned.1.call-start = ((), (), s32[]{:S(2)}) async-start(), calls=%async_computation.3 | async-start | bytes 7864320 | tf_op jit(solution)/shard_map/all_gather | solution.py:427
  10.1 97.1 %all-gather.5.cloned.1.call-start = ((), (), s32[]{:S(2)}) async-start(), calls=%async_computation.4 | async-start | bytes 7864320 | tf_op jit(solution)/shard_map/all_gather | solution.py:428
  10.8 359.5 %reduce-scatter.8.cloned.1.call-start = ((), (), s32[]{:S(2)}) async-start(), calls=%async_computation.5 | async-start | bytes 1966080 | tf_op jit(solution)/shard_map/reduce_scatter | solution.py:481
  16.0 47.6 %copy-start.23 = (f32[1536]{0:T(1024)S(1)}, f32[1536]{0:T(1024)}, u32[]{:S(2)}) copy-start(f32[1536]{0:T(1024)} %param.19) | copy-start | bytes 18436
  59.3 4.6 copy-start.11
  65.4 12.6 %copy-start.10 = (bf16[2048,1536]{0,1:T(8,128)(2,1)}, bf16[2048,1536]{0,1:T(8,128)(2,1)S(1)}, u32[]{:S(2)}) copy-start(bf16[2048,1536]{0,1:T(8,128)(2,1)S(1)} %fusion.2) | copy-start | bytes 18874372
  70.7 7.4 %copy-start.31 = (bf16[1536,768]{1,0:T(8,128)(2,1)S(1)}, bf16[1536,768]{1,0:T(8,128)(2,1)}, u32[]{:S(2)}) copy-start(bf16[1536,768]{1,0:T(8,128)(2,1)} %param.21) | copy-start | bytes 7077892
  85.3 31.8 %copy-start.7 = (f32[4,768]{1,0:T(4,128)S(1)}, f32[4,768]{1,0:T(4,128)}, u32[]{:S(2)}) copy-start(f32[4,768]{1,0:T(4,128)} %kern_ref.3) | copy-start | bytes 36868
  85.3 31.8 %copy-start.8 = (f32[4,256]{1,0:T(4,128)S(1)}, f32[4,256]{1,0:T(4,128)}, u32[]{:S(2)}) copy-start(f32[4,256]{1,0:T(4,128)} %win_ref.3) | copy-start | bytes 12292
  85.3 31.8 %copy-start.9 = (f32[256]{0:T(256)S(1)}, f32[256]{0:T(256)}, u32[]{:S(2)}) copy-start(f32[256]{0:T(256)} %param.27) | copy-start | bytes 3076
  107.2 9.9 %copy-start.1 = (f32[2048,16]{1,0:T(8,128)S(1)}, f32[2048,16]{1,0:T(8,128)}, u32[]{:S(2)}) copy-start(f32[2048,16]{1,0:T(8,128)} %pad.17.col_ref) | copy-start | bytes 393220
  107.2 9.9 %copy-start.2 = (bf16[256,768]{1,0:T(8,128)(2,1)S(1)}, bf16[256,768]{1,0:T(8,128)(2,1)}, u32[]{:S(2)}) copy-start(bf16[256,768]{1,0:T(8,128)(2,1)} %pad_maximum_fusion.ind_ref) | copy-start | bytes 1179652
  220.8 266.9 %all-reduce.13.cloned.1.call-start = ((), (), s32[]{:S(2)}) async-start(), calls=%async_computation.9 | async-start | bytes 14155776 | tf_op jit(solution)/shard_map/psum | solution.py:465
  220.8 9.5 %copy-start.22 = (f32[1,2048]{1,0:T(1,128)S(1)}, f32[1,2048]{1,0:T(1,128)}, u32[]{:S(2)}) copy-start(f32[1,2048]{1,0:T(1,128)} %copy-done.21) | copy-start | bytes 24580
  230.3 6.0 copy-start.29
  230.3 16.5 %slice-start = ((s8[6291456]{0:T(1024)(128)(4,1)}), s8[4194304]{0:T(1024)(128)(4,1)S(1)}, s32[]{:S(2)}) async-start(s8[6291456]{0:T(1024)(128)(4,1)} %bitcast.140), calls=%async_computation.10 | async-start | bytes 8388608
  236.3 10.5 %copy-start.12 = (bf16[2048,768]{1,0:T(8,128)(2,1)}, bf16[2048,768]{1,0:T(8,128)(2,1)S(1)}, u32[]{:S(2)}) copy-start(bf16[2048,768]{1,0:T(8,128)(2,1)S(1)} %multiply_convert_fusion) | copy-start | bytes 9437188
  236.3 10.5 %slice-start.1 = ((s8[6291456]{0:T(1024)(128)(4,1)}), s8[2097152]{0:T(1024)(128)(4,1)S(1)}, s32[]{:S(2)}) async-start(s8[6291456]{0:T(1024)(128)(4,1)} %bitcast.140), calls=%async_computation.11 | async-start | bytes 4194304
  253.4 294.6 %reduce-scatter.10.cloned.1.call-start = ((), (), s32[]{:S(2)}) async-start(), calls=%async_computation.6 | async-start | bytes 7864320
  271.1 338.2 %reduce-scatter.12.cloned.1.call-start = ((), (), s32[]{:S(2)}) async-start(), calls=%async_computation.7 | async-start | bytes 7864320
  272.1 6.4 copy-start.30
  272.1 6.4 copy-start.32
  278.5 8.2 %copy-start.28 = (bf16[2048,768]{1,0:T(8,128)(2,1)S(1)}, bf16[2048,768]{1,0:T(8,128)(2,1)}, u32[]{:S(2)}) copy-start(bf16[2048,768]{1,0:T(8,128)(2,1)} %get-tuple-element.29) | copy-start | bytes 9437188
  278.5 8.2 %copy-start.34 = (bf16[1536,768]{1,0:T(8,128)(2,1)S(1)}, bf16[1536,768]{1,0:T(8,128)(2,1)}, u32[]{:S(2)}) copy-start(bf16[1536,768]{1,0:T(8,128)(2,1)} %param.20) | copy-start | bytes 7077892
  286.7 8.0 %copy-start.19 = (f32[2048]{0:T(1024)S(1)}, f32[2048]{0:T(1024)}, u32[]{:S(2)}) copy-start(f32[2048]{0:T(1024)} %copy-done.18) | copy-start | bytes 24580
  286.7 8.0 %copy-start.24 = (f32[1536]{0:T(1024)S(1)}, f32[1536]{0:T(1024)}, u32[]{:S(2)}) copy-start(f32[1536]{0:T(1024)} %param.19) | copy-start | bytes 18436
  314.5 371.5 %all-reduce.11.cloned.1.call-start = ((), (), s32[]{:S(2)}) async-start(), calls=%async_computation.8 | async-start | bytes 983040 | tf_op jit(solution)/shard_map/psum | solution.py:484
  487.7 4.4 copy-start.14
  (14 other events, 29.9 us)
Sparse Core Ops, SparseCore 0:
  10.2 49.0 all-gather.2
  60.9 46.2 all-gather.4
  220.9 29.1 reduce-scatter.7
  254.8 232.8 all-reduce.12
  490.1 57.8 reduce-scatter.9
  550.4 58.8 reduce-scatter.11
  613.3 72.6 all-reduce.10
